TPU v7x, 32 devices: a whole 2x2x4 slice. The times are simulated.
32 devices in a mesh: row: 8 (over z, core), col: 4 (over y, x).
Axes of the slice: x: 2, y: 2, z: 4, core: 2. Of those that a mesh axis runs over, the one named last changes fastest.
Arguments:
- genotypes: int32 [512, 16384], P(('row', 'col')), may hold values from 0 to 2, as said below
- snp_index: int32 [512], P(('row', 'col')), may hold values from 0 to 2047, as said below
- freq_table: float32 [2048], replicated, as said below
- prior: float32 [16384, 16384], P('row', 'col'), as said below
- start_vectors: float32 [16384, 20], P('row'), may hold values from -6 to 6
Outputs:
- grm: float32 [16384, 16384], P('row', 'col')
- pcs: float32 [16384, 20], P('col')
- spectrum: float32 [3, 20], replicated
Inputs may be any that keep to these rules, and one draw needn't show every extreme that they name: `genotypes`: genotype dosages 0, 1 or 2. `snp_index`: strictly increasing; entry j lies in 4 * j to 4 * j + 3. `freq_table`: frequencies are multiples of 1/1024 between 52/1024 and 512/1024. `prior`: exactly symmetric; diagonal between 1 and 2, off-diagonal entries small.
All inputs are finite; a program needn't handle non-finite values.
Results may differ from a plain program's by a relative error of at most 0.0075.
Values may be sent and summed in bfloat16 or wider, within the bound.
A program may use at most 128 MiB of HBM per device.

v0:
```python
import jax
import jax.numpy as jnp
from jax import lax
from jax.sharding import PartitionSpec as P

S = 16384
ITERS = 3


def standardize(genotypes, allele_freq):
    doubled = 2.0 * allele_freq
    spread = jnp.sqrt(doubled * (1.0 - allele_freq))
    return (genotypes.astype(jnp.float32) - doubled[:, None]) / spread[:, None]


def orthonormal(factor, image):
    return lax.linalg.triangular_solve(factor, image, left_side=False, lower=True, transpose_a=True)


def apply_tile(tile, vectors, transposed):
    if transposed:
        return lax.dot_general(
            tile, vectors, (((0,), (0,)), ((), ())), precision=lax.Precision.HIGHEST
        )
    return jnp.dot(tile, vectors, precision=lax.Precision.HIGHEST)


def local_gram(image):
    return jnp.dot(image.T, image, precision=lax.Precision.HIGHEST)


def body(genotypes, snp_index, freq_table, prior, start_vectors):
    allele_freq = jnp.take(freq_table, snp_index)
    standard = standardize(genotypes, allele_freq).astype(jnp.bfloat16)
    row_count = lax.axis_size("row")
    col_count = lax.axis_size("col")
    own_snps = genotypes.shape[0]
    total_snps = own_snps * row_count * col_count
    row_piece = lax.all_to_all(standard, "row", split_axis=1, concat_axis=0, tiled=True)
    col_piece = lax.all_to_all(standard, "col", split_axis=1, concat_axis=0, tiled=True)
    col_piece = col_piece.reshape(col_count, 1, own_snps, col_piece.shape[1])
    col_panel = lax.all_gather(col_piece, "row", axis=1, tiled=True)
    col_panel = col_panel.reshape(total_snps, col_panel.shape[3])
    window = lax.dot_general(
        lax.all_gather(row_piece, "col", axis=0, tiled=True),
        col_panel,
        (((0,), (0,)), ((), ())),
        preferred_element_type=jnp.float32,
    )
    grm = prior + window / total_snps
    scaled_start = start_vectors / jnp.sqrt(jnp.float32(S))
    diagonals = []
    image = lax.psum(apply_tile(grm, scaled_start, True), "row")
    for step in range(1, ITERS):
        if step % 2 == 1:
            product, gram = lax.psum((apply_tile(grm, image, False), local_gram(image)), "col")
        else:
            product, gram = lax.psum((apply_tile(grm, image, True), local_gram(image)), "row")
        factor = jnp.linalg.cholesky(gram)
        diagonals.append(jnp.diagonal(factor))
        image = orthonormal(factor, product)
    gram = lax.psum(local_gram(image), "col")
    factor = jnp.linalg.cholesky(gram)
    diagonals.append(jnp.diagonal(factor))
    vectors = orthonormal(factor, image)
    pcs = vectors * jnp.sqrt(jnp.float32(S))
    spectrum = jnp.stack(diagonals, axis=0)
    return (grm, pcs, spectrum)


def solution(mesh):
    return jax.shard_map(
        body,
        mesh=mesh,
        in_specs=(P(("row", "col"), None), P(("row", "col")), P(), P("row", "col"), P("row", None)),
        out_specs=(P("row", "col"), P("col", None), P()),
        check_vma=False,
    )
```

profile of v0, /device:TPU:0, one launch (start us, length us, event | category | flops | bytes accessed | tf_op | source)
XLA Modules:
  0.0 454.8 jit_solution(4961095967382614033)
XLA Ops:
  7.2 0.7 compare_select_fusion
  8.6 0.7 broadcast_multiply_fusion
  9.2 1.4 divide_convert_fusion
  10.7 13.5 %all_to_all.35 = bf16[16,4,4096]{2,0,1:T(8,128)(2,1)S(1)} all-to-all(bf16[16,4,4096]{2,0,1:T(8,128)(2,1)S(1)} %bitcast.73), channel_id=1, replica_groups=mesh['row'=8,'col'=4] {'col'}, dimensions={1} | all-to-all | bytes 1048576 | tf_op jit(solution)/shard_map/all_to_all | solution.py:40
  24.2 1.2 copy.30
  25.5 31.8 %all_to_all.36 = bf16[16,8,2048]{2,0,1:T(8,128)(2,1)} all-to-all(bf16[16,8,2048]{2,0,1:T(8,128)(2,1)S(1)} %bitcast.72), channel_id=1, replica_groups=mesh['row'=8,'col'=4] {'row'}, dimensions={1} | all-to-all | bytes 1048576 | tf_op jit(solution)/shard_map/all_to_all | solution.py:39
  57.4 23.7 %all-gather.6.cloned.1.call-done = bf16[4,128,4096]{2,0,1:T(4,128)(2,1)} async-done(((bf16[4,16,4096]{2,0,1:T(4,128)(2,1)}), bf16[4,128,4096]{2,0,1:T(4,128)(2,1)}) %all-gather.6.cloned.1.call-update) | async-done | bytes 4194320 | tf_op jit(solution)/shard_map/all_gather | solution.py:42
  81.1 6.5 %copy.31 = bf16[4,128,4096]{2,1,0:T(8,128)(2,1)} copy(bf16[4,128,4096]{2,0,1:T(4,128)(2,1)} %all-gather.6.cloned.1.call-done) | data formatting | bytes 8388608 | tf_op jit(solution)/shard_map/all_gather | solution.py:42
  87.5 28.0 %all-gather.4.cloned.1.call-done = bf16[512,2048]{1,0:T(8,128)(2,1)} async-done(((bf16[128,2048]{1,0:T(8,128)(2,1)}), bf16[512,2048]{1,0:T(8,128)(2,1)}) %all-gather.4.cloned.1.call-update) | async-done | bytes 2097168 | tf_op jit(solution)/shard_map/all_gather | solution.py:45
  115.5 28.8 %multiply_add_fusion = f32[2048,4096]{1,0:T(8,128)} fusion(f32[2048,4096]{1,0:T(8,128)} %param.11, bf16[512,2048]{1,0:T(8,128)(2,1)} %all-gather.4.cloned.1.call-done, bf16[512,4096]{1,0:T(8,128)(2,1)} %bitcast.67), kind=kOutput, calls=%fused_computation.4 | convolution fusion | flops 8606711808 | bytes 73400320 | tf_op jit(solution)/shard_map/dot_general | solution.py:44
  144.3 22.0 %fusion.1 = f32[4096,20]{0,1:T(8,128)} fusion(f32[2048,4096]{1,0:T(8,128)} %multiply_add_fusion, f32[2048,20]{0,1:T(8,128)S(1)} %copy-done.2), kind=kOutput, calls=%fused_computation.11 | convolution fusion | flops 2013306880 | bytes 34045952 | tf_op jit(solution)/shard_map/dot_general | solution.py:22
  166.4 55.9 %all-reduce.4.cloned.1.call-done = f32[4096,20]{0,1:T(8,128)} async-done(((f32[4096,20]{0,1:T(8,128)}), f32[4096,20]{0,1:T(8,128)}) %all-reduce.4.cloned.1.call-update) | async-done | bytes 327696 | tf_op jit(solution)/shard_map/psum | solution.py:53
  222.4 1.6 fusion.27
  224.0 15.9 %psum.44 = f32[20,20]{0,1:T(8,128)S(1)} all-reduce(f32[20,20]{0,1:T(8,128)S(1)} %fusion.27), channel_id=1, replica_groups=mesh['row'=8,'col'=4] {'col'}, use_global_device_ids=true, to_apply=%region_2.3 | all-reduce | flops 400 | bytes 3200 | tf_op jit(solution)/shard_map/psum | solution.py:56
  240.0 1.8 cholesky.59
  242.5 32.6 %fusion.26 = f32[2048,20]{0,1:T(8,128)} fusion(f32[2048,4096]{1,0:T(8,128)} %multiply_add_fusion, f32[4096,20]{0,1:T(8,128)} %all-reduce.4.cloned.1.call-done), kind=kOutput, calls=%fused_computation.50 | convolution fusion | flops 2013265920 | bytes 34045952 | tf_op jit(solution)/shard_map/dot_general | solution.py:25
  275.9 1.5 custom-call.8
  277.4 0.8 gather_fusion.1
  278.2 37.0 %all-reduce.6.cloned.1.call-done = f32[2048,20]{0,1:T(8,128)} async-done(((f32[2048,20]{0,1:T(8,128)}), f32[2048,20]{0,1:T(8,128)}) %all-reduce.6.cloned.1.call-update) | async-done | bytes 163856 | tf_op jit(solution)/shard_map/psum | solution.py:56
  315.2 1.3 fusion.8
  316.8 22.0 %fusion.29 = f32[4096,20]{0,1:T(8,128)} fusion(f32[2048,4096]{1,0:T(8,128)} %multiply_add_fusion, f32[2048,20]{0,1:T(8,128)S(1)} %fusion.8), kind=kOutput, calls=%fused_computation.53 | convolution fusion | flops 2013265920 | bytes 34045952 | tf_op jit(solution)/shard_map/dot_general | solution.py:22
  338.8 28.1 %psum.45 = f32[20,20]{0,1:T(8,128)S(1)} all-reduce(f32[20,20]{0,1:T(8,128)S(1)} %fusion.28), channel_id=1, replica_groups=mesh['row'=8,'col'=4] {'row'}, use_global_device_ids=true, to_apply=%region_5.7 | all-reduce | flops 400 | bytes 3200 | tf_op jit(solution)/shard_map/psum | solution.py:58
  367.0 1.8 cholesky.70
  370.1 1.5 custom-call.16
  371.7 0.8 gather_fusion.2
  372.5 50.4 %all-reduce.8.cloned.1.call-done = f32[4096,20]{0,1:T(8,128)} async-done(((f32[4096,20]{0,1:T(8,128)}), f32[4096,20]{0,1:T(8,128)}) %all-reduce.8.cloned.1.call-update) | async-done | bytes 327696 | tf_op jit(solution)/shard_map/psum | solution.py:58
  422.9 1.5 convolution_bitcast_fusion.1
  424.9 15.9 %psum.47 = f32[20,20]{0,1:T(8,128)S(1)} all-reduce(f32[20,20]{0,1:T(8,128)S(1)} %fusion.30), channel_id=1, replica_groups=mesh['row'=8,'col'=4] {'col'}, use_global_device_ids=true, to_apply=%region_7.10 | all-reduce | flops 400 | bytes 3200 | tf_op jit(solution)/shard_map/psum | solution.py:62
  441.0 1.8 cholesky.81
  444.1 0.8 gather_fusion.3
  444.9 1.5 custom-call.17
  446.4 1.3 fusion
  (40 shorter events, 6.7 us)
Async XLA Ops:
  7.2 0.7 copy-start
  7.2 73.9 %all-gather.6.cloned.1.call-start = ((), (), s32[]{:S(2)}) async-start(), calls=%async_computation.6 | async-start | bytes 4718592 | tf_op jit(solution)/shard_map/all_gather | solution.py:42
  25.4 90.0 %all-gather.4.cloned.1.call-start = ((), (), s32[]{:S(2)}) async-start(), calls=%async_computation.2 | async-start | bytes 2621440 | tf_op jit(solution)/shard_map/all_gather | solution.py:45
  57.3 165.1 %all-reduce.4.cloned.1.call-start = ((), (), s32[]{:S(2)}) async-start(), calls=%async_computation.3 | async-start | bytes 786432 | tf_op jit(solution)/shard_map/psum | solution.py:53
  115.5 28.8 %copy-start.2 = (f32[2048,20]{0,1:T(8,128)S(1)}, f32[2048,20]{0,1:T(8,128)}, u32[]{:S(2)}) copy-start(f32[2048,20]{0,1:T(8,128)} %param.12) | copy-start | bytes 491524
  166.4 148.8 %all-reduce.6.cloned.1.call-start = ((), (), s32[]{:S(2)}) async-start(), calls=%async_computation.4 | async-start | bytes 393216 | tf_op jit(solution)/shard_map/psum | solution.py:56
  242.5 205.8 %copy-start.1 = (f32[2048]{0:T(1024)S(1)}, f32[2048]{0:T(1024)}, u32[]{:S(2)}) copy-start(f32[2048]{0:T(1024)} %param.10) | copy-start | bytes 24580
  275.2 147.7 %all-reduce.8.cloned.1.call-start = ((), (), s32[]{:S(2)}) async-start(), calls=%async_computation.5 | async-start | bytes 786432 | tf_op jit(solution)/shard_map/psum | solution.py:58
Sparse Core Ops, SparseCore 0:
  25.5 55.4 all-gather.5
  82.9 32.5 all-gather.3
  166.5 55.8 all-reduce.3
  275.3 39.8 all-reduce.5
  369.6 53.2 all-reduce.7
where the time goes:
time: 455 us
  waiting for transfers between devices  195 us (43%)
  matrix products  112 us (25%)
  blocking collectives  105 us (23%)
  other arithmetic  17.4 us (4%)
  between operations  13.9 us (3%)
  local copies, waits for them, and re-layouts  11.1 us (2%)
    psum x1, waiting for transfers between devices, body(): image = lax.psum(apply_tile(grm, scaled_start, True), 'row')  55.9 us
    psum x1, waiting for transfers between devices, body(): lax.psum((apply_tile(grm, image, True), local_gram(image)), 'row')  50.4 us
    dot_general x2, matrix products, apply_tile(): lax.dot_general(tile, vectors, (((0,), (0,)), ((), ())), precision=lax.Pr...  44.1 us
    psum x1, waiting for transfers between devices, body(): lax.psum((apply_tile(grm, image, False), local_gram(image)), 'col')  37 us
    dot_general x1, matrix products, apply_tile(): return jnp.dot(tile, vectors, precision=lax.Precision.HIGHEST)  32.6 us
    all_to_all x1, blocking collectives, body(): lax.all_to_all(standard, 'row', split_axis=1, concat_axis=0, tiled=True)  31.8 us
    dot_general x1, matrix products, body(): lax.dot_general(lax.all_gather(row_piece, 'col', axis=0, tiled=True), col...  28.8 us
    psum x1, blocking collectives, body(): lax.psum((apply_tile(grm, image, True), local_gram(image)), 'row')  28.1 us
  transfers between devices with their start and end apart: 5, of which 5 were waited for; matrix products, arithmetic and copies ran while one was open for 3% of the time, Pallas kernels for 0%

commit v1 on v0

--- a/solution.py
+++ b/solution.py
@@ -50,7 +50,7 @@
     grm = prior + window / total_snps
     scaled_start = start_vectors / jnp.sqrt(jnp.float32(S))
     diagonals = []
-    image = lax.psum(apply_tile(grm, scaled_start, True), "row")
+    image = jnp.sum(lax.all_gather(apply_tile(grm, scaled_start, True), "row"), axis=0)
     for step in range(1, ITERS):
         if step % 2 == 1:
             product, gram = lax.psum((apply_tile(grm, image, False), local_gram(image)), "col")

time: 455 us -> 441 us (0.969)
  waiting for transfers between devices: 195 us -> 177 us
    psum x1 -> x0, waiting for transfers between devices: 55.9 us -> none  [body(): image = lax.psum(apply_tile(grm, scaled_start, True), 'row')]
    all_gather x0 -> x1, waiting for transfers between devices: none -> 38.1 us  [body(): lax.all_gather(apply_tile(grm, scaled_start, True), 'row')]
where the time goes in v1:
time: 441 us; the launch traced here: 440 us
  waiting for transfers between devices  177 us (40%)
  matrix products  111 us (25%)
  blocking collectives  105 us (24%)
  other arithmetic  18 us (4%)
  local copies, waits for them, and re-layouts  14.8 us (3%)
  between operations  13.9 us (3%)
    psum x1, waiting for transfers between devices, body(): lax.psum((apply_tile(grm, image, True), local_gram(image)), 'row')  50.4 us
    dot_general x2, matrix products, apply_tile(): lax.dot_general(tile, vectors, (((0,), (0,)), ((), ())), precision=lax.Pr...  44.1 us
    all_gather x1, waiting for transfers between devices, body(): lax.all_gather(apply_tile(grm, scaled_start, True), 'row')  38.1 us
    psum x1, waiting for transfers between devices, body(): lax.psum((apply_tile(grm, image, False), local_gram(image)), 'col')  36.6 us
    dot_general x1, matrix products, apply_tile(): return jnp.dot(tile, vectors, precision=lax.Precision.HIGHEST)  32.6 us
    all_to_all x1, blocking collectives, body(): lax.all_to_all(standard, 'row', split_axis=1, concat_axis=0, tiled=True)  31.8 us
    dot_general x1, matrix products, body(): lax.dot_general(lax.all_gather(row_piece, 'col', axis=0, tiled=True), col...  28.8 us
    psum x1, blocking collectives, body(): lax.psum((apply_tile(grm, image, True), local_gram(image)), 'row')  28.1 us
  transfers between devices with their start and end apart: 5, of which 5 were waited for; matrix products, arithmetic and copies ran while one was open for 3% of the time, Pallas kernels for 0%

profile of v1, /device:TPU:0, one launch (start us, length us, event | category | flops | bytes accessed | tf_op | source)
XLA Modules:
  0.0 440.4 jit_solution(6624631494003161693)
XLA Ops:
  8.6 0.7 broadcast_multiply_fusion
  9.2 1.4 divide_convert_fusion
  10.7 13.5 %all_to_all.35 = bf16[16,4,4096]{2,0,1:T(8,128)(2,1)S(1)} all-to-all(bf16[16,4,4096]{2,0,1:T(8,128)(2,1)S(1)} %bitcast.81), channel_id=1, replica_groups=mesh['row'=8,'col'=4] {'col'}, dimensions={1} | all-to-all | bytes 1048576 | tf_op jit(solution)/shard_map/all_to_all | solution.py:40
  24.2 1.2 copy.30
  25.5 31.8 %all_to_all.36 = bf16[16,8,2048]{2,0,1:T(8,128)(2,1)} all-to-all(bf16[16,8,2048]{2,0,1:T(8,128)(2,1)S(1)} %bitcast.80), channel_id=1, replica_groups=mesh['row'=8,'col'=4] {'row'}, dimensions={1} | all-to-all | bytes 1048576 | tf_op jit(solution)/shard_map/all_to_all | solution.py:39
  57.4 23.7 %all-gather.8.cloned.1.call-done = bf16[4,128,4096]{2,0,1:T(4,128)(2,1)} async-done(((bf16[4,16,4096]{2,0,1:T(4,128)(2,1)}), bf16[4,128,4096]{2,0,1:T(4,128)(2,1)}) %all-gather.8.cloned.1.call-update) | async-done | bytes 4194320 | tf_op jit(solution)/shard_map/all_gather | solution.py:42
  81.1 6.5 %copy.31 = bf16[4,128,4096]{2,1,0:T(8,128)(2,1)} copy(bf16[4,128,4096]{2,0,1:T(4,128)(2,1)} %all-gather.8.cloned.1.call-done) | data formatting | bytes 8388608 | tf_op jit(solution)/shard_map/all_gather | solution.py:42
  87.5 28.0 %all-gather.6.cloned.1.call-done = bf16[512,2048]{1,0:T(8,128)(2,1)} async-done(((bf16[128,2048]{1,0:T(8,128)(2,1)}), bf16[512,2048]{1,0:T(8,128)(2,1)}) %all-gather.6.cloned.1.call-update) | async-done | bytes 2097168 | tf_op jit(solution)/shard_map/all_gather | solution.py:45
  115.5 28.8 %multiply_add_fusion = f32[2048,4096]{1,0:T(8,128)} fusion(f32[2048,4096]{1,0:T(8,128)} %param.11, bf16[512,2048]{1,0:T(8,128)(2,1)} %all-gather.6.cloned.1.call-done, bf16[512,4096]{1,0:T(8,128)(2,1)} %bitcast.73), kind=kOutput, calls=%fused_computation.4 | convolution fusion | flops 8606711808 | bytes 73400320 | tf_op jit(solution)/shard_map/dot_general | solution.py:44
  144.3 22.0 %fusion.1 = f32[4096,20]{0,1:T(8,128)} fusion(f32[2048,4096]{1,0:T(8,128)} %multiply_add_fusion, f32[2048,20]{0,1:T(8,128)S(1)} %copy-done.2), kind=kOutput, calls=%fused_computation.12 | convolution fusion | flops 2013306880 | bytes 34045952 | tf_op jit(solution)/shard_map/dot_general | solution.py:22
  166.6 38.1 %all-gather.10.cloned.1.call-done = f32[32768,20]{0,1:T(8,128)} async-done(((f32[4096,20]{0,1:T(8,128)}), f32[32768,20]{0,1:T(8,128)}) %all-gather.10.cloned.1.call-update) | async-done | bytes 2621456 | tf_op jit(solution)/shard_map/all_gather | solution.py:53
  204.7 3.7 copy.43
  208.5 0.7 bitcast_reduce_fusion
  209.7 32.6 %fusion.26 = f32[2048,20]{0,1:T(8,128)} fusion(f32[2048,4096]{1,0:T(8,128)} %multiply_add_fusion, f32[4096,20]{0,1:T(8,128)S(1)} %bitcast_reduce_fusion), kind=kOutput, calls=%fused_computation.51 | convolution fusion | flops 2013265920 | bytes 34045952 | tf_op jit(solution)/shard_map/dot_general | solution.py:25
  242.3 15.9 %psum.36 = f32[20,20]{0,1:T(8,128)S(1)} all-reduce(f32[20,20]{0,1:T(8,128)S(1)} %fusion.27), channel_id=1, replica_groups=mesh['row'=8,'col'=4] {'col'}, use_global_device_ids=true, to_apply=%region_2.3 | all-reduce | flops 400 | bytes 3200 | tf_op jit(solution)/shard_map/psum | solution.py:56
  258.3 1.8 cholesky.59
  261.8 1.5 custom-call.8
  263.3 0.8 gather_fusion.1
  264.1 36.6 %all-reduce.3.cloned.1.call-done = f32[2048,20]{0,1:T(8,128)} async-done(((f32[2048,20]{0,1:T(8,128)}), f32[2048,20]{0,1:T(8,128)}) %all-reduce.3.cloned.1.call-update) | async-done | bytes 163856 | tf_op jit(solution)/shard_map/psum | solution.py:56
  300.7 1.3 fusion.8
  302.3 22.0 %fusion.29 = f32[4096,20]{0,1:T(8,128)} fusion(f32[2048,4096]{1,0:T(8,128)} %multiply_add_fusion, f32[2048,20]{0,1:T(8,128)S(1)} %fusion.8), kind=kOutput, calls=%fused_computation.54 | convolution fusion | flops 2013265920 | bytes 34045952 | tf_op jit(solution)/shard_map/dot_general | solution.py:22
  324.3 28.1 %psum.37 = f32[20,20]{0,1:T(8,128)S(1)} all-reduce(f32[20,20]{0,1:T(8,128)S(1)} %fusion.28), channel_id=1, replica_groups=mesh['row'=8,'col'=4] {'row'}, use_global_device_ids=true, to_apply=%region_5.7 | all-reduce | flops 400 | bytes 3200 | tf_op jit(solution)/shard_map/psum | solution.py:58
  352.5 1.8 cholesky.70
  355.7 1.5 custom-call.16
  357.2 0.8 gather_fusion.2
  358.0 50.4 %all-reduce.5.cloned.1.call-done = f32[4096,20]{0,1:T(8,128)} async-done(((f32[4096,20]{0,1:T(8,128)}), f32[4096,20]{0,1:T(8,128)}) %all-reduce.5.cloned.1.call-update) | async-done | bytes 327696 | tf_op jit(solution)/shard_map/psum | solution.py:58
  408.4 1.5 convolution_bitcast_fusion.1
  410.5 15.9 %psum.39 = f32[20,20]{0,1:T(8,128)S(1)} all-reduce(f32[20,20]{0,1:T(8,128)S(1)} %fusion.30), channel_id=1, replica_groups=mesh['row'=8,'col'=4] {'col'}, use_global_device_ids=true, to_apply=%region_7.10 | all-reduce | flops 400 | bytes 3200 | tf_op jit(solution)/shard_map/psum | solution.py:62
  426.5 1.8 cholesky.81
  429.6 0.8 gather_fusion.3
  430.4 1.5 custom-call.17
  432.0 1.3 fusion
  (42 shorter events, 8.3 us)
Async XLA Ops:
  7.2 0.7 copy-start
  7.2 73.9 %all-gather.8.cloned.1.call-start = ((), (), s32[]{:S(2)}) async-start(), calls=%async_computation.5 | async-start | bytes 4718592 | tf_op jit(solution)/shard_map/all_gather | solution.py:42
  25.4 90.0 %all-gather.6.cloned.1.call-start = ((), (), s32[]{:S(2)}) async-start(), calls=%async_computation.2 | async-start | bytes 2621440 | tf_op jit(solution)/shard_map/all_gather | solution.py:45
  57.3 147.4 %all-gather.10.cloned.1.call-start = ((), (), s32[]{:S(2)}) async-start(), calls=%async_computation.6 | async-start | bytes 3538944 | tf_op jit(solution)/shard_map/all_gather | solution.py:53
  115.5 28.8 %copy-start.2 = (f32[2048,20]{0,1:T(8,128)S(1)}, f32[2048,20]{0,1:T(8,128)}, u32[]{:S(2)}) copy-start(f32[2048,20]{0,1:T(8,128)} %param.12) | copy-start | bytes 491524
  166.4 134.3 %all-reduce.3.cloned.1.call-start = ((), (), s32[]{:S(2)}) async-start(), calls=%async_computation.3 | async-start | bytes 393216 | tf_op jit(solution)/shard_map/psum | solution.py:56
  209.7 224.2 %copy-start.1 = (f32[2048]{0:T(1024)S(1)}, f32[2048]{0:T(1024)}, u32[]{:S(2)}) copy-start(f32[2048]{0:T(1024)} %param.10) | copy-start | bytes 24580
  260.9 147.6 %all-reduce.5.cloned.1.call-start = ((), (), s32[]{:S(2)}) async-start(), calls=%async_computation.4 | async-start | bytes 786432 | tf_op jit(solution)/shard_map/psum | solution.py:58
Sparse Core Ops, SparseCore 0:
  25.5 55.4 all-gather.7
  82.9 32.5 all-gather.5
  166.5 38.1 all-gather.9
  261.0 39.6 all-reduce.2
  355.1 53.2 all-reduce.4
